TPU v7x, 32 devices: a whole 2x2x4 slice. The times are simulated.
32 devices in a mesh: depth: 2 (over x), row: 4 (over y, core), col: 4 (over z).
Axes of the slice: x: 2, y: 2, z: 4, core: 2. Of those that a mesh axis runs over, the one named last changes fastest.
Arguments:
- q_slab: float32 [1536, 1024], P('col', ('depth', 'row')), may hold values from -6 to 6
- triangle: float32 [1024, 1024], P(None, 'depth'), as said below
- panel_q: float32 [32768, 1024], P('row', ('depth', 'col')), may hold values from -0.1875 to 0.1875
Outputs:
- slab_out: float32 [1536, 32768], P('col', 'row')
Inputs may be any that keep to these rules, and one draw needn't show every extreme that they name: triangle is zero below its diagonal; its diagonal lies in 0.5 to 1.5.
All inputs are finite; a program needn't handle non-finite values.
Results may differ from a plain program's by a relative error of at most 0.000071.
Values sent between devices are 32-bit elements; how exact they have to be, the bound alone decides.
A program may use at most 64 MiB of HBM per device.

v0:
```python
import jax
import jax.numpy as jnp
from jax import lax
from jax.sharding import PartitionSpec as P


def per_device(q_slab, triangle, panel_q):
    rows = q_slab.shape[0]
    width = triangle.shape[1]
    share = width // lax.axis_size("row")
    factor = lax.dynamic_slice_in_dim(triangle, lax.axis_index("row") * share, share, 1)
    left = jnp.dot(
        lax.all_gather(q_slab, ("depth", "row"), axis=1, tiled=True),
        factor,
        precision=lax.Precision.HIGHEST,
        preferred_element_type=jnp.float32,
    )
    left = lax.all_gather(left, "row", axis=1, tiled=True)
    narrow = panel_q.shape[1]
    columns = lax.axis_size("col")
    mixed = lax.all_to_all(panel_q, "depth", split_axis=0, concat_axis=1, tiled=True)
    left_all = lax.all_gather(left, "depth", axis=1, tiled=True)
    grid = left_all.reshape(rows, 2, columns, narrow)
    piece = lax.all_gather(mixed, "col", axis=1, tiled=True)
    count = piece.shape[1] // (2 * narrow)
    pieces = piece.reshape(piece.shape[0], count, 2, narrow)
    partial_out = jnp.einsum(
        "sdnw,rndw->sr",
        grid,
        pieces,
        precision=lax.Precision.HIGHEST,
        preferred_element_type=jnp.float32,
    )
    return lax.all_gather(partial_out, "depth", axis=1, tiled=True)


def solution(mesh):
    placed = (P("col", ("depth", "row")), P(None, "depth"), P("row", ("depth", "col")))
    return jax.shard_map(
        per_device, mesh=mesh, in_specs=placed, out_specs=P("col", "row"), check_vma=False
    )
```

profile of v0, /device:TPU:0, one launch (start us, length us, event | category | flops | bytes accessed | tf_op | source)
XLA Modules:
  0.0 567.0 jit_solution(8736152346896375355)
XLA Ops:
  6.5 0.0 copy-start
  6.5 0.0 all-gather.5.cloned.1.call-start
  6.5 0.7 all-gather.5.cloned.1.call-update
  7.3 5.6 all-to-all-start
  12.9 0.0 all-gather.7.cloned.1.call-start
  12.9 31.0 %all-gather.5.cloned.1.call-done = f32[384,1024]{1,0:T(8,128)} async-done(((f32[384,128]{1,0:T(8,128)}), f32[384,1024]{1,0:T(8,128)}) %all-gather.5.cloned.1.call-update) | async-done | bytes 1572880 | tf_op jit(solution)/shard_map/all_gather | solution.py:13
  44.0 0.0 copy-done
  44.0 3.3 convolution_bitcast_fusion
  47.3 9.1 %all_gather.16 = f32[384,512]{0,1:T(8,128)} all-gather(f32[384,128]{0,1:T(8,128)S(1)} %convolution_bitcast_fusion), channel_id=1, replica_groups=mesh['depth'=2,'row'=4,'col'=4] {'row'}, dimensions={1}, use_global_device_ids=true | all-gather | bytes 983040 | tf_op jit(solution)/shard_map/all_gather | solution.py:18
  56.4 0.0 all-gather.7.cloned.1.call-update
  56.4 0.0 all-gather.9.cloned.1.call-start
  56.5 13.7 %all-to-all-done = f32[2,4096,128]{2,1,0:T(8,128)} async-done(((f32[2,4096,128]{2,1,0:T(8,128)}), f32[2,4096,128]{2,1,0:T(8,128)}, u32[]{:S(2)}, u32[]{:S(2)}) %all-to-all-start) | async-done | bytes 4194336 | tf_op jit(solution)/shard_map/all_to_all | solution.py:21
  70.2 5.6 copy.7
  75.8 0.0 all-gather.9.cloned.1.call-update
  75.8 0.0 all-gather.11.cloned.1.call-start
  75.8 9.2 %all-gather.7.cloned.1.call-done = f32[384,1024]{0,1:T(8,128)} async-done(((f32[384,512]{0,1:T(8,128)}), f32[384,1024]{0,1:T(8,128)}) %all-gather.7.cloned.1.call-update) | async-done | bytes 1572880 | tf_op jit(solution)/shard_map/all_gather | solution.py:22
  85.1 288.9 %all-gather.9.cloned.1.call-done = f32[4096,1024]{0,1:T(8,128)} async-done(((f32[4096,256]{0,1:T(8,128)}), f32[4096,1024]{0,1:T(8,128)}) %all-gather.9.cloned.1.call-update) | async-done | bytes 16777232 | tf_op jit(solution)/shard_map/all_gather | solution.py:24
  374.0 24.7 %fusion.2 = f32[384,4096]{1,0:T(8,128)} fusion(f32[384,2,4,128]{0,3,2,1:T(8,128)} %bitcast.16, f32[4096,4,2,128]{0,3,2,1:T(8,128)} %bitcast.13), kind=kOutput, calls=%fused_computation.2 | convolution fusion | flops 19327352832 | bytes 24641536 | tf_op jit(solution)/shard_map/sdnw,rndw->sr/dot_general | solution.py:27
  398.7 0.0 all-gather.11.cloned.1.call-update
  398.7 150.8 %all-gather.11.cloned.1.call-done = f32[384,8192]{1,0:T(8,128)} async-done(((f32[384,4096]{1,0:T(8,128)}), f32[384,8192]{1,0:T(8,128)}) %all-gather.11.cloned.1.call-update) | async-done | bytes 12582928 | tf_op jit(solution)/shard_map/all_gather | solution.py:34
  549.6 0.0 copy-start.1
  549.6 10.9 %copy.19 = f32[384,8192]{1,0:T(8,128)} copy(f32[384,8192]{1,0:T(8,128)} %all-gather.11.cloned.1.call-done) | data formatting | bytes 25165824
  560.5 0.0 copy-done.1
Async XLA Ops:
  6.5 37.4 %copy-start = (f32[1024,512]{1,0:T(8,128)S(1)}, f32[1024,512]{1,0:T(8,128)}, u32[]{:S(2)}) copy-start(f32[1024,512]{1,0:T(8,128)} %param.4) | copy-start | bytes 6291460
  6.5 37.4 %all-gather.5.cloned.1.call-start = ((), (), s32[]{:S(2)}) async-start(), calls=%async_computation.1 | async-start | bytes 1769472 | tf_op jit(solution)/shard_map/all_gather | solution.py:13
  7.3 62.9 %all-to-all-start = ((f32[2,4096,128]{2,1,0:T(8,128)}), f32[2,4096,128]{2,1,0:T(8,128)}, u32[]{:S(2)}, u32[]{:S(2)}) async-start(f32[2,4096,128]{2,1,0:T(8,128)} %bitcast.15), calls=%async_computation | async-start | bytes 8388608 | tf_op jit(solution)/shard_map/all_to_all | solution.py:21
  12.9 72.2 %all-gather.7.cloned.1.call-start = ((), (), s32[]{:S(2)}) async-start(), calls=%async_computation.2 | async-start | bytes 2359296 | tf_op jit(solution)/shard_map/all_gather | solution.py:22
  56.4 317.6 %all-gather.9.cloned.1.call-start = ((), (), s32[]{:S(2)}) async-start(), calls=%async_computation.3 | async-start | bytes 20971520 | tf_op jit(solution)/shard_map/all_gather | solution.py:24
  75.8 473.8 %all-gather.11.cloned.1.call-start = ((), (), s32[]{:S(2)}) async-start(), calls=%async_computation.4 | async-start | bytes 18874368 | tf_op jit(solution)/shard_map/all_gather | solution.py:34
  549.6 10.9 %copy-start.1 = (f32[1024,512]{1,0:T(8,128)S(1)}, f32[1024,512]{1,0:T(8,128)}, u32[]{:S(2)}) copy-start(f32[1024,512]{1,0:T(8,128)} %param.4) | copy-start | bytes 6291460
Sparse Core Ops, SparseCore 0:
  9.2 34.7 all-gather.4
  56.6 28.4 all-gather.6
  86.6 287.3 all-gather.8
  398.8 150.6 all-gather.10
where the time goes:
time: 567 us
  waiting for transfers between devices  494 us (87%)
  matrix products  28 us (5%)
  local copies, waits for them, and re-layouts  16.5 us (3%)
  between operations  13.1 us (2%)
  blocking collectives  9.12 us (2%)
  starting transfers between devices  5.74 us (1%)
    all_gather x1, waiting for transfers between devices, per_device(): piece = lax.all_gather(mixed, 'col', axis=1, tiled=True)  289 us
    all_gather x1, waiting for transfers between devices, per_device(): return lax.all_gather(partial_out, 'depth', axis=1, tiled=True)  151 us
    all_gather x1, waiting for transfers between devices, per_device(): lax.all_gather(q_slab, ('depth', 'row'), axis=1, tiled=True)  31 us
    dot_general x1, matrix products, per_device(): jnp.einsum('sdnw,rndw->sr', grid, pieces, precision=lax.Precision.HIGHEST...  24.7 us
    all_to_all x1, waiting for transfers between devices, per_device(): lax.all_to_all(panel_q, 'depth', split_axis=0, concat_axis=1, tiled=True)  13.7 us
  transfers between devices with their start and end apart: 5, of which 5 were waited for; matrix products, arithmetic and copies ran while one was open for 2% of the time, Pallas kernels for 0%

commit v1 on v0

--- a/solution.py
+++ b/solution.py
@@ -1,21 +1,244 @@
+import functools
+
 import jax
 import jax.numpy as jnp
 from jax import lax
+from jax.experimental import pallas as pl
+from jax.experimental.pallas import tpu as pltpu
 from jax.sharding import PartitionSpec as P
 
-
-def per_device(q_slab, triangle, panel_q):
-    rows = q_slab.shape[0]
+MESH = pl.DeviceIdType.MESH
+CHUNK = 256
+AHEAD = 5
+
+
+def split(x):
+    high = x.astype(jnp.bfloat16)
+    return high, (x - high.astype(jnp.float32)).astype(jnp.bfloat16)
+
+
+def product(left, right):
+    return lax.dot_general(
+        left, right, (((1,), (1,)), ((), ())), preferred_element_type=jnp.float32
+    )
+
+
+def kernel(
+    cols, half, panel, high_ref, low_ref, out, buf, made, part, got,
+    own_sem, xs, xr, zs, zr, ps, pr, os, orr, ol,
+):
+    d, r, c = lax.axis_index("depth"), lax.axis_index("row"), lax.axis_index("col")
+    steps = half // CHUNK
+    slab = made.shape[1]
+    last = cols - 1
+    other = (1 - d, r, c)
+    right = (d, r, (c + 1) % cols)
+    left = (d, r, (c + cols - 1) % cols)
+
+    def rows(start, k):
+        return pl.ds(pl.multiple_of(start + k * CHUNK, CHUNK), CHUNK)
+
+    def remote(src, dst, send, recv, to):
+        return pltpu.make_async_remote_copy(
+            src_ref=src, dst_ref=dst, send_sem=send, recv_sem=recv,
+            device_id=to, device_id_type=MESH,
+        )
+
+    def swap(k, lane):
+        return remote(
+            panel.at[rows((1 - d) * half, k), :],
+            buf.at[c, lane, rows(0, k), :],
+            xs.at[k], xr.at[k], other,
+        )
+
+    def pass_on(way, b, k):
+        ref = buf.at[b, :, rows(0, k), :]
+        return remote(ref, ref, zs.at[way, b, k], zr.at[b, k], (right, left)[way])
+
+    def send_part(way, k):
+        return remote(part.at[k], got.at[k], ps.at[k], pr.at[k], (right, left)[way])
+
+    def give(k, side):
+        return remote(
+            made.at[k], out.at[:, rows(side * half, k)], os.at[k], orr.at[k], other
+        )
+
+    def keep(k):
+        return pltpu.make_async_copy(made.at[k], out.at[:, rows(d * half, k)], ol.at[k])
+
+    own = pltpu.make_async_copy(
+        panel.at[pl.ds(pl.multiple_of(d * half, half), half), :], buf.at[c, d], own_sem
+    )
+    own.start()
+
+    @pl.loop(0, steps)
+    def _(k):
+        swap(k, d).start()
+
+    own.wait()
+
+    def forward(k):
+        swap(k, 1 - d).wait_recv()
+
+        @pl.when(c < last - 1)
+        def _():
+            pass_on(0, c, k).start()
+
+        @pl.when(c > 1)
+        def _():
+            pass_on(1, c, k).start()
+
+        for b in range(cols):
+
+            @pl.when((b < c) & (c < last - 1))
+            def _():
+                pass_on(0, b, k).wait_recv()
+                pass_on(0, b, k).start()
+
+            @pl.when((b > c) & (c > 1))
+            def _():
+                pass_on(1, b, k).wait_recv()
+                pass_on(1, b, k).start()
+
+    def block(b, k):
+        x = jnp.concatenate([buf[b, 0, rows(0, k), :], buf[b, 1, rows(0, k), :]], axis=1)
+        return split(x)
+
+    inner = (c >= 1) & (c <= last - 1)
+
+    def compute(k):
+        @pl.when(inner)
+        def _():
+            for b in range(cols):
+
+                @pl.when(((b < c) & (c >= last - 1)) | ((b > c) & (c <= 1)))
+                def _():
+                    pass_on(0, b, k).wait_recv()
+
+            total = None
+            for b in range(cols):
+                high, low = block(b, k)
+                term = product(high_ref[b], high) + product(high_ref[b], low)
+                term = term + product(low_ref[b], high)
+                total = term if total is None else total + term
+            made[k] = total[:slab]
+            part[k] = total[slab:]
+
+            @pl.when(c == 1)
+            def _():
+                send_part(1, k).start()
+
+            @pl.when(c == last - 1)
+            def _():
+                send_part(0, k).start()
+
+        @pl.when((c == 0) | (c == last))
+        def _():
+            high, low = block(c, k)
+            left_high, left_low = high_ref[c, :slab], low_ref[c, :slab]
+            total = product(left_high, high) + product(left_high, low)
+            total = total + product(left_low, high)
+            send_part(0, k).wait_recv()
+            made[k] = total + got[k]
+
+        give(k, d).start()
+        keep(k).start()
+
+    @pl.loop(0, min(AHEAD, steps))
+    def _(k):
+        forward(k)
+
+    @pl.loop(0, steps)
+    def _(k):
+        @pl.when(k + AHEAD < steps)
+        def _():
+            forward(k + AHEAD)
+
+        compute(k)
+
+    @pl.loop(0, steps)
+    def _(k):
+        swap(k, d).wait_send()
+        for b in range(cols):
+
+            @pl.when((b <= c) & (c < last - 1))
+            def _():
+                pass_on(0, b, k).wait_send()
+
+            @pl.when((b >= c) & (c > 1))
+            def _():
+                pass_on(1, b, k).wait_send()
+
+        @pl.when((c == 1) | (c == last - 1))
+        def _():
+            send_part(0, k).wait_send()
+
+        keep(k).wait()
+        give(k, d).wait_send()
+        give(k, 1 - d).wait_recv()
+
+
+def lefts(q_slab, triangle):
     width = triangle.shape[1]
     share = width // lax.axis_size("row")
     factor = lax.dynamic_slice_in_dim(triangle, lax.axis_index("row") * share, share, 1)
-    left = jnp.dot(
+    return jnp.dot(
         lax.all_gather(q_slab, ("depth", "row"), axis=1, tiled=True),
         factor,
         precision=lax.Precision.HIGHEST,
         preferred_element_type=jnp.float32,
     )
-    left = lax.all_gather(left, "row", axis=1, tiled=True)
+
+
+def lined(q_slab, triangle, panel_q):
+    slab = q_slab.shape[0]
+    total_rows, narrow = panel_q.shape
+    half = total_rows // 2
+    steps = half // CHUNK
+    cols = lax.axis_size("col")
+    c = lax.axis_index("col")
+    share = lefts(q_slab, triangle)
+    beside = lax.ppermute(share, "col", [(0, 1), (cols - 1, cols - 2)])
+    both = jnp.concatenate([share, beside], axis=0)
+    both = lax.all_gather(both, ("depth", "row"), axis=1, tiled=True)
+    grid = both.reshape(2, slab, 2, cols, narrow).transpose(3, 0, 1, 2, 4)
+    at = jnp.arange(cols)
+    end = jnp.where(c == 1, 0, cols - 1)
+    mask = jnp.stack([jnp.ones_like(at, bool), at != end], axis=1)
+    grid = jnp.where(mask[:, :, None, None, None], grid, 0.0)
+    grid = grid.reshape(cols, 2 * slab, 2 * narrow)
+    high = lax.reduce_precision(grid, 8, 7)
+    low = (grid - high).astype(jnp.bfloat16)
+    high = high.astype(jnp.bfloat16)
+    dma = pltpu.SemaphoreType.DMA
+    piece = pltpu.VMEM((steps, slab, CHUNK), jnp.float32)
+    return pl.pallas_call(
+        functools.partial(kernel, cols, half),
+        out_shape=jax.ShapeDtypeStruct((slab, total_rows), jnp.float32),
+        in_specs=[
+            pl.BlockSpec(memory_space=pl.ANY),
+            pl.BlockSpec(memory_space=pltpu.VMEM),
+            pl.BlockSpec(memory_space=pltpu.VMEM),
+        ],
+        out_specs=pl.BlockSpec(memory_space=pl.ANY),
+        scratch_shapes=[
+            pltpu.VMEM((cols, 2, half, narrow), jnp.float32),
+            piece, piece, piece,
+            dma, dma((steps,)), dma((steps,)),
+            dma((2, cols, steps)), dma((cols, steps)),
+            dma((steps,)), dma((steps,)),
+            dma((steps,)), dma((steps,)), dma((steps,)),
+        ],
+        compiler_params=pltpu.CompilerParams(
+            has_side_effects=True, vmem_limit_bytes=60 * 1024 * 1024
+        ),
+        name="back_transform",
+    )(panel_q, high, low)
+
+
+def gathered(q_slab, triangle, panel_q):
+    rows = q_slab.shape[0]
+    left = lax.all_gather(lefts(q_slab, triangle), "row", axis=1, tiled=True)
     narrow = panel_q.shape[1]
     columns = lax.axis_size("col")
     mixed = lax.all_to_all(panel_q, "depth", split_axis=0, concat_axis=1, tiled=True)
@@ -34,6 +257,15 @@
     return lax.all_gather(partial_out, "depth", axis=1, tiled=True)
 
 
+def per_device(q_slab, triangle, panel_q):
+    rows, narrow = panel_q.shape
+    held = 4 * rows * (narrow * lax.axis_size("col") + 2 * q_slab.shape[0])
+    fits = held <= 48 * 1024 * 1024
+    if narrow % 128 == 0 and rows % (2 * CHUNK) == 0 and lax.axis_size("col") >= 4 and fits:
+        return lined(q_slab, triangle, panel_q)
+    return gathered(q_slab, triangle, panel_q)
+
+
 def solution(mesh):
     placed = (P("col", ("depth", "row")), P(None, "depth"), P("row", ("depth", "col")))
     return jax.shard_map(

time: 567 us -> 382 us (0.67)
  waiting for transfers between devices: 494 us -> 68.1 us
  Pallas kernels: 0 us -> 253 us
  matrix products: 28 us -> 3.34 us
  local copies, waits for them, and re-layouts: 16.5 us -> 30 us
  other arithmetic: 0 us -> 10 us
  blocking collectives: 9.12 us -> 0 us
    all_gather x4 -> x2, waiting for transfers between devices: 480 us -> 62.8 us  [the longest x1 32.3 us: lined(): both = lax.all_gather(both, ('depth', 'row'), axis=1, tiled=True)]
    pallas_call x0 -> x1, Pallas kernels: none -> 253 us  [lined(): pl.pallas_call(functools.partial(kernel, cols, half), out_shape=jax.Shape...]
    dot_general x2 -> x1, matrix products: 28 us -> 3.34 us  [lefts(): jnp.dot(lax.all_gather(q_slab, ('depth', 'row'), axis=1, tiled=True), fac...]
    reshape x0 -> x3, local copies, waits for them, and re-layouts: none -> 19.2 us  [the longest x2 13.7 us: lined(): grid = both.reshape(2, slab, 2, cols, narrow).transpose(3, 0, 1, 2, 4)]
    all_to_all x1 -> x0, waiting for transfers between devices: 13.7 us -> none  [per_device(): lax.all_to_all(panel_q, 'depth', split_axis=0, concat_axis=1, tiled=True)]
    all_gather x1 -> x0, blocking collectives: 9.12 us -> none  [per_device(): left = lax.all_gather(left, 'row', axis=1, tiled=True)]
  transfers between devices with their start and end apart: 5 -> 3, of which waited for: 5 -> 3; matrix products, arithmetic and copies ran while one was open for 2% -> 0% of each run, Pallas kernels for 0% -> 0%
where the time goes in v1:
time: 382 us; the launch traced here: 381 us
  Pallas kernels  253 us (66%)
  waiting for transfers between devices  68.1 us (18%)
  local copies, waits for them, and re-layouts  30 us (8%)
  between operations  13.4 us (4%)
  other arithmetic  10 us (3%)
    pallas_call x1, Pallas kernels, lined(): pl.pallas_call(functools.partial(kernel, cols, half), out_shape=jax.Shape...  253 us
    all_gather x1, waiting for transfers between devices, lined(): both = lax.all_gather(both, ('depth', 'row'), axis=1, tiled=True)  32.3 us
    all_gather x1, waiting for transfers between devices, lefts(): lax.all_gather(q_slab, ('depth', 'row'), axis=1, tiled=True)  30.4 us
    reshape x2, local copies, waits for them, and re-layouts, lined(): grid = both.reshape(2, slab, 2, cols, narrow).transpose(3, 0, 1, 2, 4)  13.7 us
    unnamed x3, local copies, waits for them, and re-layouts  10.8 us
  transfers between devices with their start and end apart: 3, of which 3 were waited for; matrix products, arithmetic and copies ran while one was open for 0% of the time, Pallas kernels for 0%

profile of v1, /device:TPU:0, one launch (start us, length us, event | category | flops | bytes accessed | tf_op | source)
XLA Modules:
  0.0 381.5 jit_solution(10021968394790911496)
XLA Ops:
  6.5 0.0 copy-start
  6.5 0.0 all-gather.3.cloned.1.call-start
  6.5 0.7 all-gather.3.cloned.1.call-update
  7.3 0.0 all-gather.5.cloned.1.call-start
  7.3 30.4 %all-gather.3.cloned.1.call-done = f32[384,1024]{1,0:T(8,128)} async-done(((f32[384,128]{1,0:T(8,128)}), f32[384,1024]{1,0:T(8,128)}) %all-gather.3.cloned.1.call-update) | async-done | bytes 1572880 | tf_op jit(solution)/shard_map/all_gather | solution.py:186
  37.8 0.0 copy-done
  37.8 3.3 convolution_bitcast_fusion
  41.1 3.4 collective-permute-start
  44.5 4.6 %collective-permute-done = f32[384,128]{0,1:T(8,128)S(1)} collective-permute-done((f32[384,128]{0,1:T(8,128)S(1)}, f32[384,128]{0,1:T(8,128)S(1)}, u32[]{:S(2)}, u32[]{:S(2)}) %collective-permute-start) | collective-permute-done | bytes 196640 | tf_op jit(solution)/shard_map/ppermute | solution.py:201
  49.1 0.8 pad_maximum_fusion
  49.9 0.0 all-gather.5.cloned.1.call-update
  49.9 0.1 stack.4
  50.0 32.3 %all-gather.5.cloned.1.call-done = f32[768,1024]{0,1:T(8,128)} async-done(((f32[768,128]{0,1:T(8,128)}), f32[768,1024]{0,1:T(8,128)}) %all-gather.5.cloned.1.call-update) | async-done | bytes 3145744 | tf_op jit(solution)/shard_map/all_gather | solution.py:203
  82.3 5.2 %reshape.14 = f32[2,384,2,4,128]{1,0,4,3,2:T(2,128)} reshape(f32[768,1024]{0,1:T(8,128)} %all-gather.5.cloned.1.call-done) | data formatting | bytes 6291456 | tf_op jit(solution)/shard_map/reshape | solution.py:204
  87.5 8.5 %copy.4 = f32[2,384,2,4,128]{4,2,1,0,3:T(2,128)} copy(f32[2,384,2,4,128]{1,0,4,3,2:T(2,128)} %reshape.14) | data formatting | bytes 6291456 | tf_op jit(solution)/shard_map/reshape | solution.py:204
  96.0 5.2 %bitcast_select_fusion = f32[4,2,384,2,128]{4,3,2,1,0:T(2,128)} fusion(f32[2,384,2,4,128]{4,2,1,0,3:T(2,128)} %copy.4, pred[4,2]{1,0:T(4,128)(4,1)S(1)} %stack.4), kind=kLoop, calls=%fused_computation.3 | loop fusion | flops 786432 | bytes 6291464 | tf_op jit(solution)/shard_map/jit(_where)/select_n | solution.py:208
  101.2 5.5 %reshape.15 = f32[4,768,256]{2,1,0:T(8,128)} reshape(f32[4,2,384,2,128]{4,3,2,1,0:T(2,128)} %bitcast_select_fusion) | data formatting | bytes 6291456 | tf_op jit(solution)/shard_map/reshape | solution.py:209
  106.7 4.0 %fusion = (bf16[4,768,256]{2,1,0:T(8,128)(2,1)}, bf16[4,768,256]{2,1,0:T(8,128)(2,1)}) fusion(f32[4,768,256]{2,1,0:T(8,128)} %reshape.15), kind=kLoop, calls=%fused_computation.2 | loop fusion | flops 3145728 | bytes 6291456 | tf_op jit(solution)/shard_map/convert_element_type | solution.py:211
  110.7 253.1 %back_transform.1 = f32[384,8192]{1,0:T(8,128)} custom-call(f32[8192,128]{1,0:T(8,128)} %panel.1, bf16[4,768,256]{2,1,0:T(8,128)(2,1)} %get-tuple-element.6.high_ref, bf16[4,768,256]{2,1,0:T(8,128)(2,1)} %get-tuple-element.5.low_ref), custom_call_target="tpu_custom_call" | custom-call | tf_op jit(solution)/shard_map/back_transform/pallas_call | solution.py:215
  363.9 10.8 %copy.6 = f32[384,8192]{1,0:T(8,128)} copy(f32[384,8192]{1,0:T(8,128)} %back_transform.1) | data formatting | bytes 25165824
  (1 shorter events, 0.0 us)
Async XLA Ops:
  6.5 31.2 %copy-start = (f32[1024,512]{1,0:T(8,128)S(1)}, f32[1024,512]{1,0:T(8,128)}, u32[]{:S(2)}) copy-start(f32[1024,512]{1,0:T(8,128)} %param.4) | copy-start | bytes 6291460
  6.5 31.2 %all-gather.3.cloned.1.call-start = ((), (), s32[]{:S(2)}) async-start(), calls=%async_computation | async-start | bytes 1769472 | tf_op jit(solution)/shard_map/all_gather | solution.py:186
  7.3 75.1 %all-gather.5.cloned.1.call-start = ((), (), s32[]{:S(2)}) async-start(), calls=%async_computation.1 | async-start | bytes 3538944 | tf_op jit(solution)/shard_map/all_gather | solution.py:203
  41.1 8.0 %collective-permute-start = (f32[384,128]{0,1:T(8,128)S(1)}, f32[384,128]{0,1:T(8,128)S(1)}, u32[]{:S(2)}, u32[]{:S(2)}) collective-permute-start(f32[384,128]{0,1:T(8,128)S(1)} %convolution_bitcast_fusion), channel_id=1, source_target_pairs={{0,1},{3,2},{4,5},{7,6},{8,9},{11,10},{12,13},{15,14},{16,17},{19,... | collective-permute-start | bytes 589832 | tf_op jit(solution)/shard_map/ppermute | solution.py:201
Sparse Core Ops, SparseCore 0:
  9.2 28.4 all-gather.2
  50.0 32.2 all-gather.4

commit v2 on v1

--- a/solution.py
+++ b/solution.py
@@ -10,6 +10,7 @@
 MESH = pl.DeviceIdType.MESH
 CHUNK = 256
 AHEAD = 5
+FIRST = 10
 
 
 def split(x):
@@ -24,8 +25,9 @@
 
 
 def kernel(
-    cols, half, panel, high_ref, low_ref, out, buf, made, part, got,
-    own_sem, xs, xr, zs, zr, ps, pr, os, orr, ol,
+    cols, half, slab_ref, factor_ref, panel, out, buf, made, part, got,
+    q_buf, t_buf, l_buf, high_ref, low_ref,
+    own_sem, xs, xr, zs, zr, ps, pr, os, orr, ol, mine, qs, qr, ls, lr, ns, nr,
 ):
     d, r, c = lax.axis_index("depth"), lax.axis_index("row"), lax.axis_index("col")
     steps = half // CHUNK
@@ -66,12 +68,58 @@
     def keep(k):
         return pltpu.make_async_copy(made.at[k], out.at[:, rows(d * half, k)], ol.at[k])
 
+    def flip(at, bit):
+        return at + bit * (1 - 2 * ((at // bit) % 2))
+
+    me = d * cols + r
+
+    def doubling(ref, send, recv):
+        stages = [[remote(ref.at[me], ref.at[me], send.at[0], recv.at[0], other)]]
+        held = [r]
+        count = 1
+        bit = cols // 2
+        while bit:
+            stage = []
+            for side in (d, 1 - d):
+                for at in held:
+                    ours = ref.at[side * cols + at]
+                    stage.append(
+                        remote(ours, ours, send.at[count], recv.at[count], (d, flip(r, bit), c))
+                    )
+                    count += 1
+            stages.append(stage)
+            held = held + [flip(at, bit) for at in held]
+            bit //= 2
+        return stages
+
+    def start(stage):
+        for copy in stage:
+            copy.start()
+
+    def arrive(stage):
+        for copy in stage:
+            copy.wait_recv()
+
     own = pltpu.make_async_copy(
         panel.at[pl.ds(pl.multiple_of(d * half, half), half), :], buf.at[c, d], own_sem
     )
+    share = t_buf.shape[1]
+    loads = [
+        pltpu.make_async_copy(slab_ref, q_buf.at[me], mine.at[0]),
+        pltpu.make_async_copy(
+            factor_ref.at[:, pl.ds(pl.multiple_of(r * share, share), share)], t_buf, mine.at[1]
+        ),
+    ]
+    loads[0].start()
     own.start()
-
-    @pl.loop(0, steps)
+    loads[1].start()
+    q_stages = doubling(q_buf, qs, qr)
+    l_stages = doubling(l_buf, ls, lr)
+    first = min(FIRST, steps)
+    loads[0].wait()
+    start(q_stages[0])
+
+    @pl.loop(0, first)
     def _(k):
         swap(k, d).start()
 
@@ -144,7 +192,79 @@
         give(k, d).start()
         keep(k).start()
 
-    @pl.loop(0, min(AHEAD, steps))
+    arrive(q_stages[0])
+    start(q_stages[1])
+    forward(0)
+    for before, after in zip(q_stages[1:], q_stages[2:] + [[]]):
+        arrive(before)
+        start(after)
+    loads[1].wait()
+    width = q_buf.shape[2]
+    total = None
+    for i in range(q_buf.shape[0]):
+        q_high, q_low = split(q_buf[i])
+        t_high, t_low = split(t_buf[i * width : (i + 1) * width, :])
+        term = jnp.dot(q_high, t_high, preferred_element_type=jnp.float32)
+        term = term + jnp.dot(q_high, t_low, preferred_element_type=jnp.float32)
+        term = term + jnp.dot(q_low, t_high, preferred_element_type=jnp.float32)
+        total = term if total is None else total + term
+    l_buf[me, :slab, :] = total
+
+    def beside(to):
+        return remote(
+            l_buf.at[me, :slab, :], l_buf.at[me, slab:, :], ns, nr, to
+        )
+
+    ends = (c == 0) | (c == last)
+    helps = (c == 1) | (c == last - 1)
+
+    @pl.when(c == 0)
+    def _():
+        beside(right).start()
+
+    @pl.when(c == last)
+    def _():
+        beside(left).start()
+
+    @pl.when((c != 1) & (c != last - 1))
+    def _():
+        l_buf[me, slab:, :] = jnp.zeros((slab, share), jnp.float32)
+
+    forward(1)
+
+    @pl.when(helps)
+    def _():
+        beside(left).wait_recv()
+
+    start(l_stages[0])
+
+    @pl.loop(first, steps)
+    def _(k):
+        swap(k, d).start()
+
+    forward(2)
+    for at, (before, after) in enumerate(zip(l_stages, l_stages[1:] + [[]])):
+        arrive(before)
+        start(after)
+        if at == 0:
+            forward(3)
+    for b in range(cols):
+        x = jnp.concatenate([l_buf[b], l_buf[cols + b]], axis=1)
+        high, low = split(x)
+        high_ref[b] = high
+        low_ref[b] = low
+
+    @pl.when(c == 1)
+    def _():
+        high_ref[0, slab:, :] = jnp.zeros((slab, 2 * share), jnp.bfloat16)
+        low_ref[0, slab:, :] = jnp.zeros((slab, 2 * share), jnp.bfloat16)
+
+    @pl.when(c == last - 1)
+    def _():
+        high_ref[last, slab:, :] = jnp.zeros((slab, 2 * share), jnp.bfloat16)
+        low_ref[last, slab:, :] = jnp.zeros((slab, 2 * share), jnp.bfloat16)
+
+    @pl.loop(4, AHEAD)
     def _(k):
         forward(k)
 
@@ -176,6 +296,14 @@
         keep(k).wait()
         give(k, d).wait_send()
         give(k, 1 - d).wait_recv()
+
+    for stage in q_stages + l_stages:
+        for copy in stage:
+            copy.wait_send()
+
+    @pl.when(ends)
+    def _():
+        beside(right).wait_send()
 
 
 def lefts(q_slab, triangle):
@@ -196,44 +324,39 @@
     half = total_rows // 2
     steps = half // CHUNK
     cols = lax.axis_size("col")
-    c = lax.axis_index("col")
-    share = lefts(q_slab, triangle)
-    beside = lax.ppermute(share, "col", [(0, 1), (cols - 1, cols - 2)])
-    both = jnp.concatenate([share, beside], axis=0)
-    both = lax.all_gather(both, ("depth", "row"), axis=1, tiled=True)
-    grid = both.reshape(2, slab, 2, cols, narrow).transpose(3, 0, 1, 2, 4)
-    at = jnp.arange(cols)
-    end = jnp.where(c == 1, 0, cols - 1)
-    mask = jnp.stack([jnp.ones_like(at, bool), at != end], axis=1)
-    grid = jnp.where(mask[:, :, None, None, None], grid, 0.0)
-    grid = grid.reshape(cols, 2 * slab, 2 * narrow)
-    high = lax.reduce_precision(grid, 8, 7)
-    low = (grid - high).astype(jnp.bfloat16)
-    high = high.astype(jnp.bfloat16)
     dma = pltpu.SemaphoreType.DMA
     piece = pltpu.VMEM((steps, slab, CHUNK), jnp.float32)
+    factor = pltpu.VMEM((cols, 2 * slab, 2 * narrow), jnp.bfloat16)
     return pl.pallas_call(
         functools.partial(kernel, cols, half),
         out_shape=jax.ShapeDtypeStruct((slab, total_rows), jnp.float32),
         in_specs=[
             pl.BlockSpec(memory_space=pl.ANY),
-            pl.BlockSpec(memory_space=pltpu.VMEM),
-            pl.BlockSpec(memory_space=pltpu.VMEM),
+            pl.BlockSpec(memory_space=pl.ANY),
+            pl.BlockSpec(memory_space=pl.ANY),
         ],
         out_specs=pl.BlockSpec(memory_space=pl.ANY),
         scratch_shapes=[
             pltpu.VMEM((cols, 2, half, narrow), jnp.float32),
             piece, piece, piece,
+            pltpu.VMEM((2 * cols, slab, narrow), jnp.float32),
+            pltpu.VMEM((2 * cols * narrow, narrow), jnp.float32),
+            pltpu.VMEM((2 * cols, 2 * slab, narrow), jnp.float32),
+            factor, factor,
             dma, dma((steps,)), dma((steps,)),
             dma((2, cols, steps)), dma((cols, steps)),
             dma((steps,)), dma((steps,)),
             dma((steps,)), dma((steps,)), dma((steps,)),
+            dma((2,)),
+            dma((2 * cols - 1,)), dma((2 * cols - 1,)),
+            dma((2 * cols - 1,)), dma((2 * cols - 1,)),
+            dma, dma,
         ],
         compiler_params=pltpu.CompilerParams(
             has_side_effects=True, vmem_limit_bytes=60 * 1024 * 1024
         ),
         name="back_transform",
-    )(panel_q, high, low)
+    )(q_slab, triangle, panel_q)
 
 
 def gathered(q_slab, triangle, panel_q):
@@ -261,7 +384,10 @@
     rows, narrow = panel_q.shape
     held = 4 * rows * (narrow * lax.axis_size("col") + 2 * q_slab.shape[0])
     fits = held <= 48 * 1024 * 1024
-    if narrow % 128 == 0 and rows % (2 * CHUNK) == 0 and lax.axis_size("col") >= 4 and fits:
+    cols = lax.axis_size("col")
+    even = cols >= 4 and cols & (cols - 1) == 0 and lax.axis_size("row") == cols
+    deep = rows % (2 * CHUNK) == 0 and rows >= 2 * CHUNK * AHEAD
+    if even and deep and narrow % 128 == 0 and fits:
         return lined(q_slab, triangle, panel_q)
     return gathered(q_slab, triangle, panel_q)
 

time: 382 us -> 304 us (0.80)
  waiting for transfers between devices: 68.1 us -> 0 us
  Pallas kernels: 253 us -> 293 us
  local copies, waits for them, and re-layouts: 30 us -> 10.8 us
  between operations: 13.4 us -> 0.01 us
  other arithmetic: 10 us -> 0 us
    all_gather x2 -> x0, waiting for transfers between devices: 62.8 us -> none  [the longest x1 32.3 us: lined(): both = lax.all_gather(both, ('depth', 'row'), axis=1, tiled=True)]
    pallas_call x1, Pallas kernels: 253 us -> 293 us  [lined(): pl.pallas_call(functools.partial(kernel, cols, half), out_shape=jax.Shape...]
    reshape x3 -> x0, local copies, waits for them, and re-layouts: 19.2 us -> none  [the longest x2 13.7 us: lined(): grid = both.reshape(2, slab, 2, cols, narrow).transpose(3, 0, 1, 2, 4)]
    select_n x1 -> x0, other arithmetic: 5.19 us -> none  [lined(): grid = jnp.where(mask[:, :, None, None, None], grid, 0.0)]
    ppermute x1 -> x0, waiting for transfers between devices: 4.63 us -> none  [lined(): beside = lax.ppermute(share, 'col', [(0, 1), (cols - 1, cols - 2)])]
    convert_element_type x1 -> x0, other arithmetic: 4.05 us -> none  [lined(): low = (grid - high).astype(jnp.bfloat16)]
    unnamed x3 -> x1, local copies, waits for them, and re-layouts: 10.8 us -> 10.8 us
  transfers between devices with their start and end apart: 3 -> 0, of which waited for: 3 -> 0; matrix products, arithmetic and copies ran while one was open for 0% -> 0% of each run, Pallas kernels for 0% -> 0%
where the time goes in v2:
time: 304 us
  Pallas kernels  293 us (96%)
  local copies, waits for them, and re-layouts  10.8 us (4%)
    pallas_call x1, Pallas kernels, lined(): pl.pallas_call(functools.partial(kernel, cols, half), out_shape=jax.Shape...  293 us
    unnamed x1, local copies, waits for them, and re-layouts  10.8 us

profile of v2, /device:TPU:0, one launch (start us, length us, event | category | flops | bytes accessed | tf_op | source)
XLA Modules:
  0.0 303.9 jit_solution(9843428425129601961)
XLA Ops:
  0.0 293.2 %back_transform.1 = f32[384,8192]{1,0:T(8,128)} custom-call(f32[384,128]{1,0:T(8,128)} %slab_ref.1, f32[1024,512]{1,0:T(8,128)} %factor_ref.1, f32[8192,128]{1,0:T(8,128)} %panel.1), custom_call_target="tpu_custom_call" | custom-call | tf_op jit(solution)/shard_map/back_transform/pallas_call | solution.py:330
  293.2 10.8 %copy.5 = f32[384,8192]{1,0:T(8,128)} copy(f32[384,8192]{1,0:T(8,128)} %back_transform.1) | data formatting | bytes 25165824

commit v3 on v2

--- a/solution.py
+++ b/solution.py
@@ -8,9 +8,9 @@
 from jax.sharding import PartitionSpec as P
 
 MESH = pl.DeviceIdType.MESH
-CHUNK = 256
-AHEAD = 5
-FIRST = 10
+CHUNK = 512
+AHEAD = 4
+FIRST = 3
 
 
 def split(x):
@@ -53,9 +53,9 @@
             xs.at[k], xr.at[k], other,
         )
 
-    def pass_on(way, b, k):
-        ref = buf.at[b, :, rows(0, k), :]
-        return remote(ref, ref, zs.at[way, b, k], zr.at[b, k], (right, left)[way])
+    def pass_on(way, at, k):
+        ref = buf.at[slice(0, at + 1) if way == 0 else slice(at, cols), :, rows(0, k), :]
+        return remote(ref, ref, zs.at[way, k], zr.at[way, k], (right, left)[way])
 
     def send_part(way, k):
         return remote(part.at[k], got.at[k], ps.at[k], pr.at[k], (right, left)[way])
@@ -128,25 +128,18 @@
     def forward(k):
         swap(k, 1 - d).wait_recv()
 
-        @pl.when(c < last - 1)
-        def _():
-            pass_on(0, c, k).start()
-
-        @pl.when(c > 1)
-        def _():
-            pass_on(1, c, k).start()
-
-        for b in range(cols):
-
-            @pl.when((b < c) & (c < last - 1))
-            def _():
-                pass_on(0, b, k).wait_recv()
-                pass_on(0, b, k).start()
-
-            @pl.when((b > c) & (c > 1))
-            def _():
-                pass_on(1, b, k).wait_recv()
-                pass_on(1, b, k).start()
+        for at in range(cols):
+
+            @pl.when(c == at)
+            def _():
+                if at < last - 1:
+                    if at > 0:
+                        pass_on(0, at - 1, k).wait_recv()
+                    pass_on(0, at, k).start()
+                if at > 1:
+                    if at < last:
+                        pass_on(1, at + 1, k).wait_recv()
+                    pass_on(1, at, k).start()
 
     def block(b, k):
         x = jnp.concatenate([buf[b, 0, rows(0, k), :], buf[b, 1, rows(0, k), :]], axis=1)
@@ -157,11 +150,13 @@
     def compute(k):
         @pl.when(inner)
         def _():
-            for b in range(cols):
-
-                @pl.when(((b < c) & (c >= last - 1)) | ((b > c) & (c <= 1)))
-                def _():
-                    pass_on(0, b, k).wait_recv()
+            @pl.when(c == last - 1)
+            def _():
+                pass_on(0, last - 2, k).wait_recv()
+
+            @pl.when(c == 1)
+            def _():
+                pass_on(1, 2, k).wait_recv()
 
             total = None
             for b in range(cols):
@@ -242,11 +237,11 @@
     def _(k):
         swap(k, d).start()
 
-    forward(2)
     for at, (before, after) in enumerate(zip(l_stages, l_stages[1:] + [[]])):
         arrive(before)
         start(after)
         if at == 0:
+            forward(2)
             forward(3)
     for b in range(cols):
         x = jnp.concatenate([l_buf[b], l_buf[cols + b]], axis=1)
@@ -279,15 +274,14 @@
     @pl.loop(0, steps)
     def _(k):
         swap(k, d).wait_send()
-        for b in range(cols):
-
-            @pl.when((b <= c) & (c < last - 1))
-            def _():
-                pass_on(0, b, k).wait_send()
-
-            @pl.when((b >= c) & (c > 1))
-            def _():
-                pass_on(1, b, k).wait_send()
+        for at in range(cols):
+
+            @pl.when(c == at)
+            def _():
+                if at < last - 1:
+                    pass_on(0, at, k).wait_send()
+                if at > 1:
+                    pass_on(1, at, k).wait_send()
 
         @pl.when((c == 1) | (c == last - 1))
         def _():
@@ -344,7 +338,7 @@
             pltpu.VMEM((2 * cols, 2 * slab, narrow), jnp.float32),
             factor, factor,
             dma, dma((steps,)), dma((steps,)),
-            dma((2, cols, steps)), dma((cols, steps)),
+            dma((2, steps)), dma((2, steps)),
             dma((steps,)), dma((steps,)),
             dma((steps,)), dma((steps,)), dma((steps,)),
             dma((2,)),

time: 304 us -> 283 us (0.931)
  Pallas kernels: 293 us -> 272 us
    pallas_call x1, Pallas kernels: 293 us -> 272 us  [lined(): pl.pallas_call(functools.partial(kernel, cols, half), out_shape=jax.Shape...]
where the time goes in v3:
time: 283 us
  Pallas kernels  272 us (96%)
  local copies, waits for them, and re-layouts  10.8 us (4%)
    pallas_call x1, Pallas kernels, lined(): pl.pallas_call(functools.partial(kernel, cols, half), out_shape=jax.Shape...  272 us
    unnamed x1, local copies, waits for them, and re-layouts  10.8 us

profile of v3, /device:TPU:0, one launch (start us, length us, event | category | flops | bytes accessed | tf_op | source)
XLA Modules:
  0.0 283.0 jit_solution(1859613503995582228)
XLA Ops:
  0.0 272.3 %back_transform.1 = f32[384,8192]{1,0:T(8,128)} custom-call(f32[384,128]{1,0:T(8,128)} %slab_ref.1, f32[1024,512]{1,0:T(8,128)} %factor_ref.1, f32[8192,128]{1,0:T(8,128)} %panel.1), custom_call_target="tpu_custom_call" | custom-call | tf_op jit(solution)/shard_map/back_transform/pallas_call | solution.py:324
  272.3 10.8 %copy.5 = f32[384,8192]{1,0:T(8,128)} copy(f32[384,8192]{1,0:T(8,128)} %back_transform.1) | data formatting | bytes 25165824
